TPU v7x, 32 devices: a whole 2x2x4 slice. The times are simulated.
32 devices in a mesh: dp: 4 (over y, x), expert: 4 (over z), tensor: 2 (over core).
Axes of the slice: x: 2, y: 2, z: 4, core: 2. Of those that a mesh axis runs over, the one named last changes fastest.
Arguments:
- out_grad: bfloat16 [2048, 3584], P(('dp', 'expert'), 'tensor'), may hold values from -6 to 6
- routes: int32 [2048, 8], P(('dp', 'expert')), may hold values from 0 to 255, all different within a row; in each aligned block of 128 rows (0 to 127, 128 to 255, ...) at most 5 rows name the same one
- probs: float32 [2048, 8], P(('dp', 'expert')), may hold values from 0.1 to 1
- gate_pre: bfloat16 [4, 4, 20, 1024], P('dp', 'expert', None, 'tensor'), may hold values from -8 to 8
- up_pre: bfloat16 [4, 4, 20, 1024], P('dp', 'expert', None, 'tensor'), may hold values from -6 to 6
- gate_weight: bfloat16 [4, 3584, 1024], P('expert', None, 'tensor'), may hold values from -0.09375 to 0.09375
- up_weight: bfloat16 [4, 3584, 1024], P('expert', None, 'tensor'), may hold values from -0.09375 to 0.09375
- down_weight: bfloat16 [4, 1024, 3584], P('expert', 'tensor', 'dp'), may hold values from -0.1875 to 0.1875
Outputs:
- input_grad: bfloat16 [2048, 3584], P(('dp', 'expert'), 'tensor')
Inputs may be any that keep to these rules, and one draw needn't show every extreme that they name: Each row names 8 different experts. In the 128 rows of one device no expert is named more than 5 times. Ids below 4 are the experts held here, expert e at index e of expert; routes to other ids leave no slot.
All inputs are finite; a program needn't handle non-finite values.
Results may differ from a plain program's by a relative error of at most 0.0072.
Values may be sent and summed in bfloat16 or wider, within the bound.
No kernel may reach another device: no remote copies, remote signals or barrier semaphores. Data moves between devices by JAX's collectives and lax.ppermute only.
A program may use at most 64 MiB of HBM per device.

v0:
```python
import functools

import jax
import jax.numpy as jnp
from jax import lax
from jax.experimental import pallas as pl
from jax.experimental.pallas import tpu as pltpu
from jax.sharding import PartitionSpec as P


CAP = 5
ROWS = 8
FEW = 8
MIB = 1 << 20


def slot_tables(block_routes, block_probs, experts, capacity):
    expert_ids = jnp.arange(experts, dtype=jnp.int32)
    matches = block_routes[:, :, None] == expert_ids[None, None, :]
    picked = jnp.sum(matches.astype(jnp.int32), axis=1)
    weight = jnp.sum(jnp.where(matches, block_probs[:, :, None], jnp.float32(0.0)), axis=1)
    before = jnp.cumsum(picked, axis=0) - picked
    rank_ids = jnp.arange(capacity, dtype=jnp.int32)
    select = (picked.T[:, None, :] == 1) & (before.T[:, None, :] == rank_ids[None, :, None])
    slot_scale = jnp.sum(jnp.where(select, weight.T[:, None, :], jnp.float32(0.0)), axis=2)
    return (select, slot_scale)


def shifted(blocks, axis):
    count = lax.axis_size(axis)
    me = lax.axis_index(axis)
    own = lax.dynamic_index_in_dim(blocks, me, 0, keepdims=False)
    arrived = []
    for step in range(1, count):
        target = lax.rem(me + step, count)
        block = lax.dynamic_index_in_dim(blocks, target, 0, keepdims=False)
        arrived.append(lax.ppermute(block, axis, [(i, (i + step) % count) for i in range(count)]))
    return own, arrived


def exchanged_whole(out_grad, routes, probs, gate_pre, up_pre, gate_weight, up_weight, down_weight):
    experts = lax.axis_size("expert")
    groups = lax.axis_size("dp")
    select, slot_scale = slot_tables(routes, probs, experts, CAP)
    slot_count = experts * CAP
    slot_table = select.reshape(slot_count, -1).astype(jnp.bfloat16)
    picked_rows = jnp.dot(slot_table, out_grad, preferred_element_type=jnp.float32)
    outgoing = (slot_scale.reshape(-1, 1) * picked_rows).astype(jnp.bfloat16)
    rows = lax.all_gather(outgoing, "tensor", axis=1, tiled=True)
    width = rows.shape[1] // groups
    blocks = rows.reshape(experts, CAP, groups, width).transpose(2, 0, 1, 3)
    blocks = blocks.reshape(groups * experts, CAP, width)
    arrived = lax.all_to_all(blocks, ("dp", "expert"), split_axis=0, concat_axis=0, tiled=True)
    part = lax.dot_general(
        arrived.reshape(groups * slot_count, width),
        down_weight[0],
        (((1,), (1,)), ((), ())),
        preferred_element_type=jnp.float32,
    )
    part = part.astype(jnp.bfloat16).reshape(groups, slot_count, -1)
    if groups <= FEW:
        own, others = shifted(part, "dp")
        hidden_grad = own.astype(jnp.float32)
        for other in others:
            hidden_grad = hidden_grad + other.astype(jnp.float32)
    else:
        part = lax.all_to_all(part, "dp", split_axis=0, concat_axis=0, tiled=True)
        hidden_grad = jnp.sum(part.astype(jnp.float32), axis=0)
    gate_act = gate_pre[0, 0].astype(jnp.float32)
    up_act = up_pre[0, 0].astype(jnp.float32)
    sigmoid_gate = jax.nn.sigmoid(gate_act)
    activated = gate_act * sigmoid_gate
    derivative = sigmoid_gate * (1.0 + gate_act * (1.0 - sigmoid_gate))
    gate_grad = (hidden_grad * up_act * derivative).astype(jnp.bfloat16)
    up_grad = (hidden_grad * activated).astype(jnp.bfloat16)

    def back(weights):
        value = lax.dot_general(
            gate_grad, weights[0], (((1,), (1,)), ((), ())), preferred_element_type=jnp.float32
        )
        return value + lax.dot_general(
            up_grad, weights[1], (((1,), (1,)), ((), ())), preferred_element_type=jnp.float32
        )

    value = back((gate_weight[0], up_weight[0])).astype(jnp.bfloat16)
    halves = lax.axis_size("tensor")
    value = value.reshape(slot_count, halves, -1).transpose(1, 0, 2)
    own, others = shifted(value, "tensor")
    slot_grad = own.astype(jnp.float32)
    for other in others:
        slot_grad = slot_grad + other.astype(jnp.float32)
    slot_grad = slot_grad.astype(jnp.bfloat16).reshape(experts, CAP, -1)
    if experts <= FEW:
        own, others = shifted(slot_grad, "expert")
        me = lax.axis_index("expert")
        table = slot_table.reshape(experts, CAP, -1)
        tables = [
            lax.dynamic_index_in_dim(table, lax.rem(me + experts - i, experts), 0, keepdims=False)
            for i in range(experts)
        ]
        tables = jnp.concatenate(tables, axis=0)
        returned = jnp.concatenate([own] + others, axis=0)
    else:
        returned = lax.all_to_all(slot_grad, "expert", split_axis=0, concat_axis=0, tiled=True)
        returned = returned.reshape(slot_count, -1)
        tables = slot_table
    combined = lax.dot_general(
        tables, returned, (((0,), (0,)), ((), ())), preferred_element_type=jnp.float32
    )
    return combined.astype(jnp.bfloat16)


HELD = pl.BlockSpec(memory_space=pltpu.VMEM)
FAR = pl.BlockSpec(memory_space=pltpu.HBM)
LOOSE = pl.BlockSpec(memory_space=pl.ANY)


def call(kernel, outs, specs, mib, scratch=()):
    return pl.pallas_call(
        kernel,
        out_shape=outs,
        in_specs=specs,
        out_specs=[HELD] * len(outs),
        scratch_shapes=list(scratch),
        compiler_params=pltpu.CompilerParams(vmem_limit_bytes=mib * MIB),
    )


def far(value):
    return pltpu.with_memory_space_constraint(value, pltpu.HBM)


def transposed(a, b):
    return lax.dot_general(a, b, (((1,), (1,)), ((), ())), preferred_element_type=jnp.float32)


def ahead(place, step, count):
    if count & (count - 1):
        return (place + step) % count if isinstance(place, int) else lax.rem(place + step, count)
    return place ^ step


def behind(place, step, count):
    return ahead(place, (count - step) if count & (count - 1) else step, count)


def dispatch_kernel(experts, routes_far, probs_far, grad_far, table_ref, *refs):
    block_refs, (routes_ref, probs_ref, grad_ref, arrived) = refs[:experts], refs[experts:]
    copies = [
        pltpu.make_async_copy(source, near, arrived.at[k])
        for k, (source, near) in enumerate(
            [(routes_far, routes_ref), (probs_far, probs_ref), (grad_far, grad_ref)]
        )
    ]
    for copy in copies:
        copy.start()
    me = lax.axis_index("expert")
    tokens = grad_ref.shape[0]
    earlier = lax.broadcasted_iota(jnp.int32, (tokens, tokens), 0) < lax.broadcasted_iota(
        jnp.int32, (tokens, tokens), 1
    )
    earlier = jnp.where(earlier, 1.0, 0.0).astype(jnp.bfloat16)
    rank = lax.broadcasted_iota(jnp.int32, (ROWS, tokens), 0)
    rank = jnp.where(rank < CAP, rank.astype(jnp.float32), -1.0)
    copies[0].wait()
    copies[1].wait()
    routes = routes_ref[...]
    probs = probs_ref[...]
    matches = [routes == ahead(me, i, experts) for i in range(experts)]
    picked = jnp.concatenate(
        [jnp.max(jnp.where(m, 1.0, 0.0), axis=0, keepdims=True) for m in matches], axis=0
    )
    before = jnp.dot(picked.astype(jnp.bfloat16), earlier, preferred_element_type=jnp.float32)
    tables, scales = [], []
    for i in range(experts):
        weight = jnp.sum(jnp.where(matches[i], probs, 0.0), axis=0, keepdims=True)
        chosen = (before[i : i + 1] == rank) & (picked[i : i + 1] > 0.5)
        tables.append(jnp.where(chosen, 1.0, 0.0))
        scales.append(jnp.sum(jnp.where(chosen, weight, 0.0), axis=1, keepdims=True))
    table = jnp.concatenate(tables, axis=0).astype(jnp.bfloat16)
    table_ref[...] = table
    copies[2].wait()
    rows = jnp.dot(table, grad_ref[...], preferred_element_type=jnp.float32)
    rows = rows * jnp.concatenate(scales, axis=0)
    for i in range(experts):
        block_refs[i][...] = rows[i * ROWS : (i + 1) * ROWS].astype(jnp.bfloat16)


def stack_kernel(*refs):
    blocks, out_ref = refs[1:-1], refs[-1]
    for j, block in enumerate(blocks):
        out_ref[j * ROWS : (j + 1) * ROWS, :] = block[...]


def column_kernel(halves, inner, *refs):
    stacks, pieces = refs[:halves], refs[halves:]
    width = pieces[0].shape[1]
    core = lax.axis_index("tensor")
    high_place, low_place = (f(lax.axis_index("dp"), inner) for f in (lax.div, lax.rem))
    for high in range(halves):
        half = ahead(high_place, high, halves)
        for turn in range(halves):

            @pl.when(half == behind(core, turn, halves))
            def _():
                for low in range(inner):
                    first = pl.multiple_of(ahead(low_place, low, inner) * width, width)
                    pieces[high * inner + low][...] = stacks[turn][:, pl.ds(first, width)]


def factor_kernel(
    experts, gate_far, up_far, down_far, after, gate_factor_ref, up_factor_ref, down_ref,
    gate_ref, up_ref, arrived,
):
    copies = [
        pltpu.make_async_copy(source, near, arrived.at[k])
        for k, (source, near) in enumerate(
            [(gate_far, gate_ref), (up_far, up_ref), (down_far, down_ref)]
        )
    ]
    for copy in copies:
        copy.start()
    me = lax.axis_index("expert")
    row = lax.broadcasted_iota(jnp.int32, (experts * ROWS, experts * CAP), 0)
    slot = lax.broadcasted_iota(jnp.int32, (experts * ROWS, experts * CAP), 1)
    rank = lax.rem(row, ROWS)
    source = behind(me, lax.div(row, ROWS), experts)
    taken = (slot == source * CAP + rank) & (rank < CAP)
    place = jnp.where(taken, 1.0, 0.0).astype(jnp.bfloat16)
    copies[0].wait()
    copies[1].wait()
    gate = jnp.dot(place, gate_ref[...], preferred_element_type=jnp.float32)
    up = jnp.dot(place, up_ref[...], preferred_element_type=jnp.float32)
    sigmoid = jax.nn.sigmoid(gate)
    gate_factor_ref[...] = up * (sigmoid * (1.0 + gate * (1.0 - sigmoid)))
    up_factor_ref[...] = gate * sigmoid
    copies[2].wait()


def fetch_kernel(far, after, near, arrived):
    copy = pltpu.make_async_copy(far, near, arrived)
    copy.start()
    copy.wait()


def hidden_kernel(*refs):
    count = len(refs) // 2 - 1
    arrived, down_ref, outs = refs[:count], refs[count], refs[count + 2 :]
    rows = arrived[0].shape[0]
    together = jnp.concatenate([a[...] for a in arrived], axis=0)
    part = transposed(together, down_ref[...])
    for k, out in enumerate(outs):
        out[...] = part[k * rows : (k + 1) * rows].astype(out.dtype)


def feature_kernel(offset, halves, *refs):
    parts, (gate_factor, up_factor, gate_weight, up_weight, out_ref) = refs[:-5], refs[-5:]
    hidden = parts[0][...].astype(jnp.float32)
    for part in parts[1:]:
        hidden = hidden + part[...].astype(jnp.float32)
    gate_grad = (hidden * gate_factor[...]).astype(jnp.bfloat16)
    up_grad = (hidden * up_factor[...]).astype(jnp.bfloat16)
    width = out_ref.shape[1]
    first = ahead(lax.axis_index("tensor"), offset, halves) * width
    span = pl.ds(pl.multiple_of(first, width), width)
    value = transposed(gate_grad, gate_weight[span, :]) + transposed(up_grad, up_weight[span, :])
    out_ref[...] = value.astype(jnp.bfloat16)


def moved(value, axis, step, back=False):
    count = lax.axis_size(axis)
    to = behind if back else ahead
    return lax.ppermute(value, axis, [(i, to(i, step, count)) for i in range(count)])


def exchanged(out_grad, routes, probs, gate_pre, up_pre, gate_weight, up_weight, down_weight):
    experts, groups, halves = (lax.axis_size(a) for a in ("expert", "dp", "tensor"))
    tokens, half = out_grad.shape
    inner = groups // halves
    hidden, width = down_weight.shape[1:]
    if experts > FEW or groups > FEW or groups % halves or half != inner * width or width % 128:
        return exchanged_whole(
            out_grad, routes, probs, gate_pre, up_pre, gate_weight, up_weight, down_weight
        )
    rows = experts * ROWS
    bf16 = functools.partial(jax.ShapeDtypeStruct, dtype=jnp.bfloat16)
    f32 = functools.partial(jax.ShapeDtypeStruct, dtype=jnp.float32)
    copies = pltpu.SemaphoreType.DMA

    table, *blocks = call(
        functools.partial(dispatch_kernel, experts),
        [bf16((rows, tokens))] + [bf16((ROWS, half))] * experts,
        [FAR] * 3,
        8,
        [
            pltpu.VMEM(routes.T.shape, routes.dtype),
            pltpu.VMEM(probs.T.shape, probs.dtype),
            pltpu.VMEM(out_grad.shape, out_grad.dtype),
            copies((3,)),
        ],
    )(far(routes.T), far(probs.T), far(out_grad))
    own = blocks[0]
    blocks = [own] + [moved(blocks[i], "expert", i) for i in range(1, experts)]
    slots = gate_pre.shape[2:]
    gate_factor, up_factor, down = call(
        functools.partial(factor_kernel, experts),
        [f32((rows, hidden))] * 2 + [bf16((hidden, width))],
        [FAR] * 3 + [LOOSE],
        8,
        [pltpu.VMEM(slots, gate_pre.dtype), pltpu.VMEM(slots, up_pre.dtype), copies((3,))],
    )(far(gate_pre[0, 0]), far(up_pre[0, 0]), far(down_weight[0]), own)
    stack = call(stack_kernel, [bf16((rows, half))], [LOOSE] + [HELD] * experts, 8)(
        gate_factor, *blocks
    )[0]
    stacks = [stack] + [moved(stack, "tensor", turn) for turn in range(1, halves)]
    pieces = call(
        functools.partial(column_kernel, halves, inner),
        [bf16((rows, width))] * groups,
        [HELD] * halves,
        8,
    )(*stacks)
    fetch = call(fetch_kernel, [bf16(gate_weight.shape[1:])], [FAR, LOOSE], 8, [copies])
    gate_held = fetch(far(gate_weight[0]), pieces[0])[0]

    def spread(values, to):
        out = [values[0]]
        for high in range(halves):
            for low in range(inner):
                if high or low:
                    pairs = []
                    for g in range(groups):
                        d = to(g // inner, high, halves) * inner + to(g % inner, low, inner)
                        pairs.append((g, d))
                    k = high * inner + low
                    out.append(lax.ppermute(values[k], "dp", pairs))
        return out

    parts = call(
        hidden_kernel,
        [f32((rows, hidden))] + [bf16((rows, hidden))] * (groups - 1),
        [HELD] * (groups + 1) + [LOOSE],
        8,
    )(*spread(pieces, ahead), down, gate_held)
    sums = spread(parts, behind)
    up_held = fetch(far(up_weight[0]), parts[-1])[0]
    shares = []
    for offset in range(halves - 1, -1, -1):
        value = call(
            functools.partial(feature_kernel, offset, halves),
            [bf16((rows, half))],
            [HELD] * (groups + 4),
            16,
        )(*sums, gate_factor, up_factor, gate_held, up_held)[0]
        shares.append(moved(value, "tensor", offset) if offset else value)
    slot_grad = sum(share.astype(jnp.float32) for share in shares).astype(jnp.bfloat16)
    returned = [slot_grad[j * ROWS : (j + 1) * ROWS] for j in range(experts)]
    returned = [returned[0]] + [
        moved(returned[j], "expert", j, back=True) for j in range(1, experts)
    ]
    combined = lax.dot_general(
        table,
        jnp.concatenate(returned, axis=0),
        (((0,), (0,)), ((), ())),
        preferred_element_type=jnp.float32,
    )
    return combined.astype(jnp.bfloat16)


def solution(mesh):
    placed = (
        P(("dp", "expert"), "tensor"),
        P(("dp", "expert"), None),
        P(("dp", "expert"), None),
        P("dp", "expert", None, "tensor"),
        P("dp", "expert", None, "tensor"),
        P("expert", None, "tensor"),
        P("expert", None, "tensor"),
        P("expert", "tensor", "dp"),
    )
    return jax.shard_map(
        exchanged, mesh=mesh, in_specs=placed, out_specs=P(("dp", "expert"), "tensor"), check_vma=False
    )
```

profile of v0, /device:TPU:0, one launch (start us, length us, event | category | flops | bytes accessed | tf_op | source)
XLA Modules:
  0.0 38.6 jit_solution(13366830322674872559)
XLA Ops:
  0.0 1.3 %shard_map.82 = (bf16[32,128]{1,0:T(8,128)(2,1)S(1)}, bf16[8,1792]{1,0:T(8,128)(2,1)S(1)}, bf16[8,1792]{1,0:T(8,128)(2,1)S(1)}, bf16[8,1792]{1,0:T(8,128)(2,1)S(1)}, bf16[8,1792]{1,0:T(8,128)(2,1)S(1)}) custom-call(s32[8,128]{1,0:T(8,128)} %bitcast.13, f32[8,128]{1,0:T(8,128)} %bitcast.14, bf16[128,1792]{1,0:T(8,128)(2,1)} %grad_far.1), custom_call_target="tpu_custom_call" | custom-call | tf_op jit(solution)/shard_map/pallas_call | solution.py:290
  1.3 3.1 %collective-permute-start = (bf16[8,1792]{1,0:T(8,128)(2,1)S(1)}, bf16[8,1792]{1,0:T(8,128)(2,1)S(1)}, u32[]{:S(2)}, u32[]{:S(2)}) collective-permute-start(bf16[8,1792]{1,0:T(8,128)(2,1)S(1)} %get-tuple-element.24), channel_id=1, source_target_pairs={{0,2},{2,0},{4,6},{6,4},{1,3},{3,1},{5,7},{7,5},{8,10},{10,8},{12,... | collective-permute-start | bytes 86024 | tf_op jit(solution)/shard_map/ppermute | solution.py:273
  4.4 2.6 %collective-permute-start.1 = (bf16[8,1792]{1,0:T(8,128)(2,1)S(1)}, bf16[8,1792]{1,0:T(8,128)(2,1)S(1)}, u32[]{:S(2)}, u32[]{:S(2)}) collective-permute-start(bf16[8,1792]{1,0:T(8,128)(2,1)S(1)} %get-tuple-element.25), channel_id=1, source_target_pairs={{0,4},{2,6},{4,0},{6,2},{1,5},{3,7},{5,1},{7,3},{8,12},{10,14},{12... | collective-permute-start | bytes 86024 | tf_op jit(solution)/shard_map/ppermute | solution.py:273
  7.0 1.2 %shard_map.83 = (f32[32,512]{1,0:T(8,128)S(1)}, f32[32,512]{1,0:T(8,128)S(1)}, bf16[512,896]{1,0:T(8,128)(2,1)S(1)}) custom-call(bf16[20,512]{1,0:T(8,128)(2,1)} %bitcast.11, bf16[20,512]{1,0:T(8,128)(2,1)} %bitcast.12, bf16[512,896]{1,0:T(8,128)(2,1)} %bitcast.10, bf16[8,1792]{1,0:T(8,128)(2,1)S(1)} %get-tuple-element.22.after.refs_1_), custom_call_target="tpu_custom_call" | custom-call | tf_op jit(solution)/shard_map/pallas_call | solution.py:305
  8.2 0.0 collective-permute-done.refs_2_
  8.3 1.4 %collective-permute-done.1.refs_3_ = bf16[8,1792]{1,0:T(8,128)(2,1)S(1)} collective-permute-done((bf16[8,1792]{1,0:T(8,128)(2,1)S(1)}, bf16[8,1792]{1,0:T(8,128)(2,1)S(1)}, u32[]{:S(2)}, u32[]{:S(2)}) %collective-permute-start.1) | collective-permute-done | bytes 28704 | tf_op jit(solution)/shard_map/ppermute | solution.py:273
  9.6 3.0 %collective-permute-done.2.refs_4_ = bf16[8,1792]{1,0:T(8,128)(2,1)S(1)} collective-permute-done((bf16[8,1792]{1,0:T(8,128)(2,1)S(1)}, bf16[8,1792]{1,0:T(8,128)(2,1)S(1)}, u32[]{:S(2)}, u32[]{:S(2)}) %collective-permute-start.2) | collective-permute-done | bytes 28704 | tf_op jit(solution)/shard_map/ppermute | solution.py:273
  12.7 0.1 collective-permute-start.3
  12.8 1.3 %collective-permute-done.3.refs_1_ = bf16[32,1792]{1,0:T(8,128)(2,1)S(1)} collective-permute-done((bf16[32,1792]{1,0:T(8,128)(2,1)S(1)}, bf16[32,1792]{1,0:T(8,128)(2,1)S(1)}, u32[]{:S(2)}, u32[]{:S(2)}) %collective-permute-start.3) | collective-permute-done | bytes 114720 | tf_op jit(solution)/shard_map/ppermute | solution.py:273
  14.1 1.6 %collective-permute-start.4 = (bf16[32,896]{1,0:T(8,128)(2,1)S(1)}, bf16[32,896]{1,0:T(8,128)(2,1)S(1)}, u32[]{:S(2)}, u32[]{:S(2)}) collective-permute-start(bf16[32,896]{1,0:T(8,128)(2,1)S(1)} %get-tuple-element.28), channel_id=1, source_target_pairs={{0,8},{8,0},{16,24},{24,16},{1,9},{9,1},{17,25},{25,17},{2,10},{10... | collective-permute-start | bytes 172040 | tf_op jit(solution)/shard_map/ppermute | solution.py:335
  15.7 1.5 %collective-permute-start.5 = (bf16[32,896]{1,0:T(8,128)(2,1)S(1)}, bf16[32,896]{1,0:T(8,128)(2,1)S(1)}, u32[]{:S(2)}, u32[]{:S(2)}) collective-permute-start(bf16[32,896]{1,0:T(8,128)(2,1)S(1)} %get-tuple-element.29), channel_id=1, source_target_pairs={{0,16},{8,24},{16,0},{24,8},{1,17},{9,25},{17,1},{25,9},{2,18},{10... | collective-permute-start | bytes 172040 | tf_op jit(solution)/shard_map/ppermute | solution.py:335
  17.2 0.5 %collective-permute-start.6 = (bf16[32,896]{1,0:T(8,128)(2,1)S(1)}, bf16[32,896]{1,0:T(8,128)(2,1)S(1)}, u32[]{:S(2)}, u32[]{:S(2)}) collective-permute-start(bf16[32,896]{1,0:T(8,128)(2,1)S(1)} %get-tuple-element.30), channel_id=1, source_target_pairs={{0,24},{8,16},{16,8},{24,0},{1,25},{9,17},{17,9},{25,1},{2,26},{10... | collective-permute-start | bytes 172040 | tf_op jit(solution)/shard_map/ppermute | solution.py:335
  17.7 2.0 %shard_map.86.refs_5_.refs_6_ = bf16[3584,512]{1,0:T(8,128)(2,1)S(1)} custom-call(bf16[3584,512]{1,0:T(8,128)(2,1)} %bitcast.9, bf16[32,896]{1,0:T(8,128)(2,1)S(1)} %get-tuple-element.27.after.refs_0_), custom_call_target="tpu_custom_call" | custom-call | tf_op jit(solution)/shard_map/pallas_call | solution.py:323
  19.7 0.1 collective-permute-done.5.refs_2_
  19.8 2.4 %collective-permute-done.6.refs_3_ = bf16[32,896]{1,0:T(8,128)(2,1)S(1)} collective-permute-done((bf16[32,896]{1,0:T(8,128)(2,1)S(1)}, bf16[32,896]{1,0:T(8,128)(2,1)S(1)}, u32[]{:S(2)}, u32[]{:S(2)}) %collective-permute-start.6) | collective-permute-done | bytes 57376 | tf_op jit(solution)/shard_map/ppermute | solution.py:335
  22.3 0.4 %shard_map.87 = (f32[32,512]{1,0:T(8,128)S(1)}, bf16[32,512]{1,0:T(8,128)(2,1)S(1)}, bf16[32,512]{1,0:T(8,128)(2,1)S(1)}, bf16[32,512]{1,0:T(8,128)(2,1)S(1)}) custom-call(bf16[32,896]{1,0:T(8,128)(2,1)S(1)} %get-tuple-element.27.after.refs_0_, bf16[32,896]{1,0:T(8,128)(2,1)S(1)} %collective-permute-done.4.refs_1_, ...), custom_call_target="tpu_custom_call" | custom-call | tf_op jit(solution)/shard_map/pallas_call | solution.py:338
  22.7 0.6 %collective-permute-start.7 = (bf16[32,512]{1,0:T(8,128)(2,1)S(1)}, bf16[32,512]{1,0:T(8,128)(2,1)S(1)}, u32[]{:S(2)}, u32[]{:S(2)}) collective-permute-start(bf16[32,512]{1,0:T(8,128)(2,1)S(1)} %get-tuple-element.33), channel_id=1, source_target_pairs={{0,8},{8,0},{16,24},{24,16},{1,9},{9,1},{17,25},{25,17},{2,10},{10... | collective-permute-start | bytes 98312 | tf_op jit(solution)/shard_map/ppermute | solution.py:335
  23.3 0.5 %collective-permute-start.8 = (bf16[32,512]{1,0:T(8,128)(2,1)S(1)}, bf16[32,512]{1,0:T(8,128)(2,1)S(1)}, u32[]{:S(2)}, u32[]{:S(2)}) collective-permute-start(bf16[32,512]{1,0:T(8,128)(2,1)S(1)} %get-tuple-element.34), channel_id=1, source_target_pairs={{0,16},{8,24},{16,0},{24,8},{1,17},{9,25},{17,1},{25,9},{2,18},{10... | collective-permute-start | bytes 98312 | tf_op jit(solution)/shard_map/ppermute | solution.py:335
  23.8 2.4 %collective-permute-start.9 = (bf16[32,512]{1,0:T(8,128)(2,1)S(1)}, bf16[32,512]{1,0:T(8,128)(2,1)S(1)}, u32[]{:S(2)}, u32[]{:S(2)}) collective-permute-start(bf16[32,512]{1,0:T(8,128)(2,1)S(1)} %get-tuple-element.35.after), channel_id=1, source_target_pairs={{0,24},{8,16},{16,8},{24,0},{1,25},{9,17},{17,9},{25,1},{2,26},{10... | collective-permute-start | bytes 98312 | tf_op jit(solution)/shard_map/ppermute | solution.py:335
  26.2 2.0 %shard_map.88.refs_7_ = bf16[3584,512]{1,0:T(8,128)(2,1)S(1)} custom-call(bf16[3584,512]{1,0:T(8,128)(2,1)} %bitcast.8, bf16[32,512]{1,0:T(8,128)(2,1)S(1)} %get-tuple-element.35.after), custom_call_target="tpu_custom_call" | custom-call | tf_op jit(solution)/shard_map/pallas_call | solution.py:345
  28.3 0.0 collective-permute-done.7.refs_1_
  28.3 0.3 collective-permute-done.9.refs_3_
  28.6 1.2 %shard_map.89 = bf16[32,1792]{1,0:T(8,128)(2,1)S(1)} custom-call(f32[32,512]{1,0:T(8,128)S(1)} %get-tuple-element.32.refs_0_, bf16[32,512]{1,0:T(8,128)(2,1)S(1)} %collective-permute-done.7.refs_1_, bf16[32,512]{1,0:T(8,128)(2,1)S(1)} %collective-permute-done.8.refs_2_, bf16[32,512]{1,0:T(8,128)(2,1)S(1)} %collective-permute-done.9.refs_3_, ...), custom_call_target="tpu_custom_call" | custom-call | tf_op jit(solution)/shard_map/pallas_call | solution.py:348
  29.8 0.0 collective-permute-start.10
  29.8 1.2 %shard_map.90 = bf16[32,1792]{1,0:T(8,128)(2,1)S(1)} custom-call(f32[32,512]{1,0:T(8,128)S(1)} %get-tuple-element.32.refs_0_, bf16[32,512]{1,0:T(8,128)(2,1)S(1)} %collective-permute-done.7.refs_1_, bf16[32,512]{1,0:T(8,128)(2,1)S(1)} %collective-permute-done.8.refs_2_, bf16[32,512]{1,0:T(8,128)(2,1)S(1)} %collective-permute-done.9.refs_3_, ...), custom_call_target="tpu_custom_call" | custom-call | tf_op jit(solution)/shard_map/pallas_call | solution.py:348
  31.0 0.1 collective-permute-done.10
  31.2 0.4 collective-permute-start.13
  31.6 4.1 %collective-permute-start.11 = (bf16[8,1792]{1,0:T(8,128)(2,1)S(1)}, bf16[8,1792]{1,0:T(8,128)(2,1)S(1)}, u32[]{:S(2)}, u32[]{:S(2)}) collective-permute-start(bf16[8,1792]{1,0:T(8,128)(2,1)S(1)} %get-tuple-element.40), channel_id=1, source_target_pairs={{0,2},{2,0},{4,6},{6,4},{1,3},{3,1},{5,7},{7,5},{8,10},{10,8},{12,... | collective-permute-start | bytes 86024 | tf_op jit(solution)/shard_map/ppermute | solution.py:273
  35.6 1.6 %collective-permute-done.13 = bf16[8,1792]{1,0:T(8,128)(2,1)S(1)} collective-permute-done((bf16[8,1792]{1,0:T(8,128)(2,1)S(1)}, bf16[8,1792]{1,0:T(8,128)(2,1)S(1)}, u32[]{:S(2)}, u32[]{:S(2)}) %collective-permute-start.13) | collective-permute-done | bytes 28704 | tf_op jit(solution)/shard_map/ppermute | solution.py:273
  37.2 0.0 collective-permute-done.12
  37.3 0.3 collective-permute-done.11
  37.6 1.1 %convolution_convert_fusion = bf16[128,1792]{1,0:T(8,128)(2,1)} fusion(bf16[32,128]{1,0:T(8,128)(2,1)S(1)} %get-tuple-element.21, bf16[8,1792]{1,0:T(8,128)(2,1)S(1)} %collective-permute-done.13, bf16[8,1792]{1,0:T(8,128)(2,1)S(1)} %collective-permute-done.12, bf16[8,1792]{1,0:T(8,128)(2,1)S(1)} %collective-permute-done.11, ...), kind=kOutput, calls=%fused_computation | convolution fusion | flops 15368192 | bytes 581632 | tf_op jit(solution)/shard_map/dot_general | solution.py:360
  (8 shorter events, 0.1 us)
Async XLA Ops:
  1.3 7.0 %collective-permute-start = (bf16[8,1792]{1,0:T(8,128)(2,1)S(1)}, bf16[8,1792]{1,0:T(8,128)(2,1)S(1)}, u32[]{:S(2)}, u32[]{:S(2)}) collective-permute-start(bf16[8,1792]{1,0:T(8,128)(2,1)S(1)} %get-tuple-element.24), channel_id=1, source_target_pairs={{0,2},{2,0},{4,6},{6,4},{1,3},{3,1},{5,7},{7,5},{8,10},{10,8},{12,... | collective-permute-start | bytes 86024 | tf_op jit(solution)/shard_map/ppermute | solution.py:273
  4.4 5.2 %collective-permute-start.1 = (bf16[8,1792]{1,0:T(8,128)(2,1)S(1)}, bf16[8,1792]{1,0:T(8,128)(2,1)S(1)}, u32[]{:S(2)}, u32[]{:S(2)}) collective-permute-start(bf16[8,1792]{1,0:T(8,128)(2,1)S(1)} %get-tuple-element.25), channel_id=1, source_target_pairs={{0,4},{2,6},{4,0},{6,2},{1,5},{3,7},{5,1},{7,3},{8,12},{10,14},{12... | collective-permute-start | bytes 86024 | tf_op jit(solution)/shard_map/ppermute | solution.py:273
  7.0 5.7 %collective-permute-start.2 = (bf16[8,1792]{1,0:T(8,128)(2,1)S(1)}, bf16[8,1792]{1,0:T(8,128)(2,1)S(1)}, u32[]{:S(2)}, u32[]{:S(2)}) collective-permute-start(bf16[8,1792]{1,0:T(8,128)(2,1)S(1)} %get-tuple-element.26), channel_id=1, source_target_pairs={{0,6},{2,4},{4,2},{6,0},{1,7},{3,5},{5,3},{7,1},{8,14},{10,12},{12... | collective-permute-start | bytes 86024 | tf_op jit(solution)/shard_map/ppermute | solution.py:273
  12.7 1.4 %collective-permute-start.3 = (bf16[32,1792]{1,0:T(8,128)(2,1)S(1)}, bf16[32,1792]{1,0:T(8,128)(2,1)S(1)}, u32[]{:S(2)}, u32[]{:S(2)}) collective-permute-start(bf16[32,1792]{1,0:T(8,128)(2,1)S(1)} %shard_map.84.refs_0_), channel_id=1, source_target_pairs={{0,1},{1,0},{2,3},{3,2},{4,5},{5,4},{6,7},{7,6},{8,9},{9,8},{10,11... | collective-permute-start | bytes 344072 | tf_op jit(solution)/shard_map/ppermute | solution.py:273
  14.1 5.6 %collective-permute-start.4 = (bf16[32,896]{1,0:T(8,128)(2,1)S(1)}, bf16[32,896]{1,0:T(8,128)(2,1)S(1)}, u32[]{:S(2)}, u32[]{:S(2)}) collective-permute-start(bf16[32,896]{1,0:T(8,128)(2,1)S(1)} %get-tuple-element.28), channel_id=1, source_target_pairs={{0,8},{8,0},{16,24},{24,16},{1,9},{9,1},{17,25},{25,17},{2,10},{10... | collective-permute-start | bytes 172040 | tf_op jit(solution)/shard_map/ppermute | solution.py:335
  15.7 4.2 %collective-permute-start.5 = (bf16[32,896]{1,0:T(8,128)(2,1)S(1)}, bf16[32,896]{1,0:T(8,128)(2,1)S(1)}, u32[]{:S(2)}, u32[]{:S(2)}) collective-permute-start(bf16[32,896]{1,0:T(8,128)(2,1)S(1)} %get-tuple-element.29), channel_id=1, source_target_pairs={{0,16},{8,24},{16,0},{24,8},{1,17},{9,25},{17,1},{25,9},{2,18},{10... | collective-permute-start | bytes 172040 | tf_op jit(solution)/shard_map/ppermute | solution.py:335
  17.2 5.1 %collective-permute-start.6 = (bf16[32,896]{1,0:T(8,128)(2,1)S(1)}, bf16[32,896]{1,0:T(8,128)(2,1)S(1)}, u32[]{:S(2)}, u32[]{:S(2)}) collective-permute-start(bf16[32,896]{1,0:T(8,128)(2,1)S(1)} %get-tuple-element.30), channel_id=1, source_target_pairs={{0,24},{8,16},{16,8},{24,0},{1,25},{9,17},{17,9},{25,1},{2,26},{10... | collective-permute-start | bytes 172040 | tf_op jit(solution)/shard_map/ppermute | solution.py:335
  22.7 5.6 %collective-permute-start.7 = (bf16[32,512]{1,0:T(8,128)(2,1)S(1)}, bf16[32,512]{1,0:T(8,128)(2,1)S(1)}, u32[]{:S(2)}, u32[]{:S(2)}) collective-permute-start(bf16[32,512]{1,0:T(8,128)(2,1)S(1)} %get-tuple-element.33), channel_id=1, source_target_pairs={{0,8},{8,0},{16,24},{24,16},{1,9},{9,1},{17,25},{25,17},{2,10},{10... | collective-permute-start | bytes 98312 | tf_op jit(solution)/shard_map/ppermute | solution.py:335
  23.3 5.0 %collective-permute-start.8 = (bf16[32,512]{1,0:T(8,128)(2,1)S(1)}, bf16[32,512]{1,0:T(8,128)(2,1)S(1)}, u32[]{:S(2)}, u32[]{:S(2)}) collective-permute-start(bf16[32,512]{1,0:T(8,128)(2,1)S(1)} %get-tuple-element.34), channel_id=1, source_target_pairs={{0,16},{8,24},{16,0},{24,8},{1,17},{9,25},{17,1},{25,9},{2,18},{10... | collective-permute-start | bytes 98312 | tf_op jit(solution)/shard_map/ppermute | solution.py:335
  23.8 4.8 %collective-permute-start.9 = (bf16[32,512]{1,0:T(8,128)(2,1)S(1)}, bf16[32,512]{1,0:T(8,128)(2,1)S(1)}, u32[]{:S(2)}, u32[]{:S(2)}) collective-permute-start(bf16[32,512]{1,0:T(8,128)(2,1)S(1)} %get-tuple-element.35.after), channel_id=1, source_target_pairs={{0,24},{8,16},{16,8},{24,0},{1,25},{9,17},{17,9},{25,1},{2,26},{10... | collective-permute-start | bytes 98312 | tf_op jit(solution)/shard_map/ppermute | solution.py:335
  29.8 1.4 %collective-permute-start.10 = (bf16[32,1792]{1,0:T(8,128)(2,1)S(1)}, bf16[32,1792]{1,0:T(8,128)(2,1)S(1)}, u32[]{:S(2)}, u32[]{:S(2)}) collective-permute-start(bf16[32,1792]{1,0:T(8,128)(2,1)S(1)} %shard_map.89), channel_id=1, source_target_pairs={{0,1},{1,0},{2,3},{3,2},{4,5},{5,4},{6,7},{7,6},{8,9},{9,8},{10,11... | collective-permute-start | bytes 344072 | tf_op jit(solution)/shard_map/ppermute | solution.py:273
  31.2 6.0 %collective-permute-start.13 = (bf16[8,1792]{1,0:T(8,128)(2,1)S(1)}, bf16[8,1792]{1,0:T(8,128)(2,1)S(1)}, u32[]{:S(2)}, u32[]{:S(2)}) collective-permute-start(bf16[8,1792]{1,0:T(8,128)(2,1)S(1)} %get-tuple-element.38), channel_id=1, source_target_pairs={{0,6},{2,4},{4,2},{6,0},{1,7},{3,5},{5,3},{7,1},{8,14},{10,12},{12... | collective-permute-start | bytes 86024 | tf_op jit(solution)/shard_map/ppermute | solution.py:273
  31.6 5.7 %collective-permute-start.12 = (bf16[8,1792]{1,0:T(8,128)(2,1)S(1)}, bf16[8,1792]{1,0:T(8,128)(2,1)S(1)}, u32[]{:S(2)}, u32[]{:S(2)}) collective-permute-start(bf16[8,1792]{1,0:T(8,128)(2,1)S(1)} %get-tuple-element.39), channel_id=1, source_target_pairs={{0,4},{2,6},{4,0},{6,2},{1,5},{3,7},{5,1},{7,3},{8,12},{10,14},{12... | collective-permute-start | bytes 86024 | tf_op jit(solution)/shard_map/ppermute | solution.py:273
  31.6 6.0 %collective-permute-start.11 = (bf16[8,1792]{1,0:T(8,128)(2,1)S(1)}, bf16[8,1792]{1,0:T(8,128)(2,1)S(1)}, u32[]{:S(2)}, u32[]{:S(2)}) collective-permute-start(bf16[8,1792]{1,0:T(8,128)(2,1)S(1)} %get-tuple-element.40), channel_id=1, source_target_pairs={{0,2},{2,0},{4,6},{6,4},{1,3},{3,1},{5,7},{7,5},{8,10},{10,8},{12,... | collective-permute-start | bytes 86024 | tf_op jit(solution)/shard_map/ppermute | solution.py:273
where the time goes:
time: 38.9 us; the launch traced here: 38.6 us
  starting transfers between devices  17.4 us (45%)
  waiting for transfers between devices  10.6 us (27%)
  Pallas kernels  9.42 us (24%)
  matrix products  1.08 us (3%)
    ppermute x8, starting transfers between devices, moved(): lax.ppermute(value, axis, [(i, to(i, step, count)) for i in range(count)])  10.3 us
    ppermute x8, waiting for transfers between devices, moved(): lax.ppermute(value, axis, [(i, to(i, step, count)) for i in range(count)])  7.78 us
    ppermute x6, starting transfers between devices, spread(): out.append(lax.ppermute(values[k], 'dp', pairs))  7.11 us
    ppermute x6, waiting for transfers between devices, spread(): out.append(lax.ppermute(values[k], 'dp', pairs))  2.84 us
    pallas_call x2, Pallas kernels, exchanged(): call(functools.partial(feature_kernel, offset, halves), [bf16((rows, half...  2.33 us
    pallas_call x1, Pallas kernels, exchanged(): gate_held = fetch(far(gate_weight[0]), pieces[0])[0]  2.05 us
    pallas_call x1, Pallas kernels, exchanged(): up_held = fetch(far(up_weight[0]), parts[-1])[0]  2.05 us
    pallas_call x1, Pallas kernels, exchanged(): call(functools.partial(dispatch_kernel, experts), [bf16((rows, tokens))]...  1.28 us
  transfers between devices with their start and end apart: 14, of which 9 were waited for; matrix products, arithmetic and copies ran while one was open for 0% of the time, Pallas kernels for 17%

commit v1 on v0

--- a/solution.py
+++ b/solution.py
@@ -134,16 +134,6 @@
     return lax.dot_general(a, b, (((1,), (1,)), ((), ())), preferred_element_type=jnp.float32)
 
 
-def ahead(place, step, count):
-    if count & (count - 1):
-        return (place + step) % count if isinstance(place, int) else lax.rem(place + step, count)
-    return place ^ step
-
-
-def behind(place, step, count):
-    return ahead(place, (count - step) if count & (count - 1) else step, count)
-
-
 def dispatch_kernel(experts, routes_far, probs_far, grad_far, table_ref, *refs):
     block_refs, (routes_ref, probs_ref, grad_ref, arrived) = refs[:experts], refs[experts:]
     copies = [
@@ -166,7 +156,7 @@
     copies[1].wait()
     routes = routes_ref[...]
     probs = probs_ref[...]
-    matches = [routes == ahead(me, i, experts) for i in range(experts)]
+    matches = [routes == (me ^ i) for i in range(experts)]
     picked = jnp.concatenate(
         [jnp.max(jnp.where(m, 1.0, 0.0), axis=0, keepdims=True) for m in matches], axis=0
     )
@@ -192,20 +182,24 @@
         out_ref[j * ROWS : (j + 1) * ROWS, :] = block[...]
 
 
-def column_kernel(halves, inner, *refs):
-    stacks, pieces = refs[:halves], refs[halves:]
+def column_kernel(inner, own, other, *pieces):
     width = pieces[0].shape[1]
-    core = lax.axis_index("tensor")
-    high_place, low_place = (f(lax.axis_index("dp"), inner) for f in (lax.div, lax.rem))
-    for high in range(halves):
-        half = ahead(high_place, high, halves)
-        for turn in range(halves):
-
-            @pl.when(half == behind(core, turn, halves))
-            def _():
-                for low in range(inner):
-                    first = pl.multiple_of(ahead(low_place, low, inner) * width, width)
-                    pieces[high * inner + low][...] = stacks[turn][:, pl.ds(first, width)]
+    core, place = lax.axis_index("tensor"), lax.axis_index("dp")
+    rest = slice(ROWS, own.shape[0])
+    for k, piece in enumerate(pieces):
+        holder = place ^ k
+        first = pl.multiple_of(lax.rem(holder, inner) * width, width)
+        span = pl.ds(first, width)
+
+        @pl.when(lax.div(holder, inner) == core)
+        def _():
+            piece[:ROWS, :] = own[:ROWS, span]
+            piece[rest, :] = other[rest, span]
+
+        @pl.when(lax.div(holder, inner) != core)
+        def _():
+            piece[:ROWS, :] = other[:ROWS, span]
+            piece[rest, :] = own[rest, span]
 
 
 def factor_kernel(
@@ -224,7 +218,7 @@
     row = lax.broadcasted_iota(jnp.int32, (experts * ROWS, experts * CAP), 0)
     slot = lax.broadcasted_iota(jnp.int32, (experts * ROWS, experts * CAP), 1)
     rank = lax.rem(row, ROWS)
-    source = behind(me, lax.div(row, ROWS), experts)
+    source = me ^ lax.div(row, ROWS)
     taken = (slot == source * CAP + rank) & (rank < CAP)
     place = jnp.where(taken, 1.0, 0.0).astype(jnp.bfloat16)
     copies[0].wait()
@@ -244,16 +238,17 @@
 
 
 def hidden_kernel(*refs):
-    count = len(refs) // 2 - 1
-    arrived, down_ref, outs = refs[:count], refs[count], refs[count + 2 :]
+    count = (len(refs) - 3) // 2
+    arrived, (down, other_down), outs = refs[:count], refs[count : count + 2], refs[count + 3 :]
     rows = arrived[0].shape[0]
-    together = jnp.concatenate([a[...] for a in arrived], axis=0)
-    part = transposed(together, down_ref[...])
-    for k, out in enumerate(outs):
+    together = jnp.concatenate([a[...] for a in arrived[1:]], axis=0)
+    part = transposed(together, other_down[...])
+    for k, out in enumerate(outs[1:]):
         out[...] = part[k * rows : (k + 1) * rows].astype(out.dtype)
-
-
-def feature_kernel(offset, halves, *refs):
+    outs[0][...] = transposed(arrived[0][...], down[...])
+
+
+def feature_kernel(offset, *refs):
     parts, (gate_factor, up_factor, gate_weight, up_weight, out_ref) = refs[:-5], refs[-5:]
     hidden = parts[0][...].astype(jnp.float32)
     for part in parts[1:]:
@@ -261,16 +256,26 @@
     gate_grad = (hidden * gate_factor[...]).astype(jnp.bfloat16)
     up_grad = (hidden * up_factor[...]).astype(jnp.bfloat16)
     width = out_ref.shape[1]
-    first = ahead(lax.axis_index("tensor"), offset, halves) * width
+    first = (lax.axis_index("tensor") ^ offset) * width
     span = pl.ds(pl.multiple_of(first, width), width)
     value = transposed(gate_grad, gate_weight[span, :]) + transposed(up_grad, up_weight[span, :])
     out_ref[...] = value.astype(jnp.bfloat16)
 
 
-def moved(value, axis, step, back=False):
-    count = lax.axis_size(axis)
-    to = behind if back else ahead
-    return lax.ppermute(value, axis, [(i, to(i, step, count)) for i in range(count)])
+def swapped(value):
+    return lax.ppermute(value, "tensor", [(0, 1), (1, 0)])
+
+
+def crossed(values, axis):
+    out = [values[0]]
+    for k in range(1, len(values)):
+        pairs = [(i * 2 + t, (i ^ k) * 2 + 1 - t) for i in range(len(values)) for t in range(2)]
+        out.append(lax.ppermute(values[k], (axis, "tensor"), pairs))
+    return out
+
+
+def suits(experts, groups, halves):
+    return all(n <= FEW and n & (n - 1) == 0 for n in (experts, groups)) and halves == 2 <= groups
 
 
 def exchanged(out_grad, routes, probs, gate_pre, up_pre, gate_weight, up_weight, down_weight):
@@ -278,7 +283,7 @@
     tokens, half = out_grad.shape
     inner = groups // halves
     hidden, width = down_weight.shape[1:]
-    if experts > FEW or groups > FEW or groups % halves or half != inner * width or width % 128:
+    if not suits(experts, groups, halves) or half != inner * width or width % 128:
         return exchanged_whole(
             out_grad, routes, probs, gate_pre, up_pre, gate_weight, up_weight, down_weight
         )
@@ -300,7 +305,8 @@
         ],
     )(far(routes.T), far(probs.T), far(out_grad))
     own = blocks[0]
-    blocks = [own] + [moved(blocks[i], "expert", i) for i in range(1, experts)]
+    blocks = crossed(blocks, "expert")
+    other_down = swapped(down_weight[0])
     slots = gate_pre.shape[2:]
     gate_factor, up_factor, down = call(
         functools.partial(factor_kernel, experts),
@@ -312,51 +318,33 @@
     stack = call(stack_kernel, [bf16((rows, half))], [LOOSE] + [HELD] * experts, 8)(
         gate_factor, *blocks
     )[0]
-    stacks = [stack] + [moved(stack, "tensor", turn) for turn in range(1, halves)]
     pieces = call(
-        functools.partial(column_kernel, halves, inner),
-        [bf16((rows, width))] * groups,
-        [HELD] * halves,
-        8,
-    )(*stacks)
+        functools.partial(column_kernel, inner), [bf16((rows, width))] * groups, [HELD] * 2, 8
+    )(stack, swapped(stack))
     fetch = call(fetch_kernel, [bf16(gate_weight.shape[1:])], [FAR, LOOSE], 8, [copies])
     gate_held = fetch(far(gate_weight[0]), pieces[0])[0]
-
-    def spread(values, to):
-        out = [values[0]]
-        for high in range(halves):
-            for low in range(inner):
-                if high or low:
-                    pairs = []
-                    for g in range(groups):
-                        d = to(g // inner, high, halves) * inner + to(g % inner, low, inner)
-                        pairs.append((g, d))
-                    k = high * inner + low
-                    out.append(lax.ppermute(values[k], "dp", pairs))
-        return out
 
     parts = call(
         hidden_kernel,
         [f32((rows, hidden))] + [bf16((rows, hidden))] * (groups - 1),
-        [HELD] * (groups + 1) + [LOOSE],
+        [HELD] * (groups + 2) + [LOOSE],
         8,
-    )(*spread(pieces, ahead), down, gate_held)
-    sums = spread(parts, behind)
+    )(*crossed(pieces, "dp"), down, other_down, gate_held)
+    sums = crossed(parts, "dp")
     up_held = fetch(far(up_weight[0]), parts[-1])[0]
     shares = []
-    for offset in range(halves - 1, -1, -1):
+    for offset in range(halves):
         value = call(
-            functools.partial(feature_kernel, offset, halves),
+            functools.partial(feature_kernel, offset),
             [bf16((rows, half))],
             [HELD] * (groups + 4),
             16,
         )(*sums, gate_factor, up_factor, gate_held, up_held)[0]
-        shares.append(moved(value, "tensor", offset) if offset else value)
+        shares.append(value if offset else swapped(value))
     slot_grad = sum(share.astype(jnp.float32) for share in shares).astype(jnp.bfloat16)
     returned = [slot_grad[j * ROWS : (j + 1) * ROWS] for j in range(experts)]
-    returned = [returned[0]] + [
-        moved(returned[j], "expert", j, back=True) for j in range(1, experts)
-    ]
+    returned = crossed(returned, "expert")
+    returned[0] = swapped(returned[0])
     combined = lax.dot_general(
         table,
         jnp.concatenate(returned, axis=0),
@@ -377,6 +365,10 @@
         P("expert", None, "tensor"),
         P("expert", "tensor", "dp"),
     )
-    return jax.shard_map(
+    step = jax.shard_map(
         exchanged, mesh=mesh, in_specs=placed, out_specs=P(("dp", "expert"), "tensor"), check_vma=False
     )
+    experts, groups = mesh.shape["expert"], mesh.shape["dp"]
+    if not suits(experts, groups, mesh.shape["tensor"]):
+        return step
+    return step

time: 38.9 us -> 37.6 us (0.967)
  waiting for transfers between devices: 10.6 us -> 9.6 us
  starting transfers between devices: 17.4 us -> 16.9 us
    ppermute x14 -> x16, waiting for transfers between devices: 10.6 us -> 9.6 us  [the longest x12 8.61 us: crossed(): out.append(lax.ppermute(values[k], (axis, 'tensor'), pairs))]
    ppermute x14 -> x16, starting transfers between devices: 17.4 us -> 16.9 us  [the longest x12 15.3 us: crossed(): out.append(lax.ppermute(values[k], (axis, 'tensor'), pairs))]
  transfers between devices with their start and end apart: 14 -> 16, of which waited for: 9 -> 7; matrix products, arithmetic and copies ran while one was open for 0% -> 0% of each run, Pallas kernels for 17% -> 21%
where the time goes in v1:
time: 37.6 us; the launch traced here: 37.4 us
  starting transfers between devices  16.9 us (45%)
  Pallas kernels  9.64 us (26%)
  waiting for transfers between devices  9.6 us (26%)
  matrix products  1.08 us (3%)
    ppermute x12, starting transfers between devices, crossed(): out.append(lax.ppermute(values[k], (axis, 'tensor'), pairs))  15.3 us
    ppermute x12, waiting for transfers between devices, crossed(): out.append(lax.ppermute(values[k], (axis, 'tensor'), pairs))  8.61 us
    pallas_call x2, Pallas kernels, exchanged(): call(functools.partial(feature_kernel, offset), [bf16((rows, half))], [HE...  2.34 us
    pallas_call x1, Pallas kernels, exchanged(): gate_held = fetch(far(gate_weight[0]), pieces[0])[0]  2.05 us
    pallas_call x1, Pallas kernels, exchanged(): up_held = fetch(far(up_weight[0]), parts[-1])[0]  2.05 us
    ppermute x4, starting transfers between devices, swapped(): return lax.ppermute(value, 'tensor', [(0, 1), (1, 0)])  1.67 us
    pallas_call x1, Pallas kernels, exchanged(): call(functools.partial(dispatch_kernel, experts), [bf16((rows, tokens))]...  1.28 us
    pallas_call x1, Pallas kernels, exchanged(): call(functools.partial(factor_kernel, experts), [f32((rows, hidden))] * 2...  1.24 us
  transfers between devices with their start and end apart: 16, of which 7 were waited for; matrix products, arithmetic and copies ran while one was open for 0% of the time, Pallas kernels for 21%

profile of v1, /device:TPU:0, one launch (start us, length us, event | category | flops | bytes accessed | tf_op | source)
XLA Modules:
  0.0 37.4 jit_solution(8697934769273504221)
XLA Ops:
  0.0 0.5 %collective-permute-start.7 = (bf16[512,896]{1,0:T(8,128)(2,1)}, bf16[512,896]{1,0:T(8,128)(2,1)S(1)}, u32[]{:S(2)}, u32[]{:S(2)}) collective-permute-start(bf16[512,896]{1,0:T(8,128)(2,1)} %bitcast.10), channel_id=1, source_target_pairs={{0,1},{1,0},{2,3},{3,2},{4,5},{5,4},{6,7},{7,6},{8,9},{9,8},{10,11... | collective-permute-start | bytes 2752520 | tf_op jit(solution)/shard_map/ppermute | solution.py:266
  0.5 1.3 %shard_map.82 = (bf16[32,128]{1,0:T(8,128)(2,1)S(1)}, bf16[8,1792]{1,0:T(8,128)(2,1)S(1)}, bf16[8,1792]{1,0:T(8,128)(2,1)S(1)}, bf16[8,1792]{1,0:T(8,128)(2,1)S(1)}, bf16[8,1792]{1,0:T(8,128)(2,1)S(1)}) custom-call(s32[8,128]{1,0:T(8,128)} %bitcast.14, f32[8,128]{1,0:T(8,128)} %bitcast.15, bf16[128,1792]{1,0:T(8,128)(2,1)} %grad_far.1), custom_call_target="tpu_custom_call" | custom-call | tf_op jit(solution)/shard_map/pallas_call | solution.py:295
  1.8 2.7 %collective-permute-start = (bf16[8,1792]{1,0:T(8,128)(2,1)S(1)}, bf16[8,1792]{1,0:T(8,128)(2,1)S(1)}, u32[]{:S(2)}, u32[]{:S(2)}) collective-permute-start(bf16[8,1792]{1,0:T(8,128)(2,1)S(1)} %get-tuple-element.24), channel_id=1, source_target_pairs={{0,3},{1,2},{2,1},{3,0},{4,7},{5,6},{6,5},{7,4},{8,11},{9,10},{10,... | collective-permute-start | bytes 86024 | tf_op jit(solution)/shard_map/ppermute | solution.py:273
  4.5 2.2 %collective-permute-start.1 = (bf16[8,1792]{1,0:T(8,128)(2,1)S(1)}, bf16[8,1792]{1,0:T(8,128)(2,1)S(1)}, u32[]{:S(2)}, u32[]{:S(2)}) collective-permute-start(bf16[8,1792]{1,0:T(8,128)(2,1)S(1)} %get-tuple-element.25), channel_id=1, source_target_pairs={{0,5},{1,4},{2,7},{3,6},{4,1},{5,0},{6,3},{7,2},{8,13},{9,12},{10,... | collective-permute-start | bytes 86024 | tf_op jit(solution)/shard_map/ppermute | solution.py:273
  6.7 0.0 collective-permute-start.2
  6.7 1.2 %shard_map.83 = (f32[32,512]{1,0:T(8,128)S(1)}, f32[32,512]{1,0:T(8,128)S(1)}, bf16[512,896]{1,0:T(8,128)(2,1)S(1)}) custom-call(bf16[20,512]{1,0:T(8,128)(2,1)} %bitcast.12, bf16[20,512]{1,0:T(8,128)(2,1)} %bitcast.13, bf16[512,896]{1,0:T(8,128)(2,1)} %bitcast.11, bf16[8,1792]{1,0:T(8,128)(2,1)S(1)} %get-tuple-element.22.after.refs_1_), custom_call_target="tpu_custom_call" | custom-call | tf_op jit(solution)/shard_map/pallas_call | solution.py:311
  8.0 0.0 collective-permute-done.refs_2_
  8.0 1.2 %collective-permute-done.1.refs_3_ = bf16[8,1792]{1,0:T(8,128)(2,1)S(1)} collective-permute-done((bf16[8,1792]{1,0:T(8,128)(2,1)S(1)}, bf16[8,1792]{1,0:T(8,128)(2,1)S(1)}, u32[]{:S(2)}, u32[]{:S(2)}) %collective-permute-start.1) | collective-permute-done | bytes 28704 | tf_op jit(solution)/shard_map/ppermute | solution.py:273
  9.2 2.6 %collective-permute-done.2.refs_4_ = bf16[8,1792]{1,0:T(8,128)(2,1)S(1)} collective-permute-done((bf16[8,1792]{1,0:T(8,128)(2,1)S(1)}, bf16[8,1792]{1,0:T(8,128)(2,1)S(1)}, u32[]{:S(2)}, u32[]{:S(2)}) %collective-permute-start.2) | collective-permute-done | bytes 28704 | tf_op jit(solution)/shard_map/ppermute | solution.py:273
  11.8 0.6 %collective-permute-start.3 = (bf16[32,1792]{1,0:T(8,128)(2,1)S(1)}, bf16[32,1792]{1,0:T(8,128)(2,1)S(1)}, u32[]{:S(2)}, u32[]{:S(2)}) collective-permute-start(bf16[32,1792]{1,0:T(8,128)(2,1)S(1)} %shard_map.84.own), channel_id=1, source_target_pairs={{0,1},{1,0},{2,3},{3,2},{4,5},{5,4},{6,7},{7,6},{8,9},{9,8},{10,11... | collective-permute-start | bytes 344072 | tf_op jit(solution)/shard_map/ppermute | solution.py:266
  12.4 1.0 %collective-permute-done.3.other = bf16[32,1792]{1,0:T(8,128)(2,1)S(1)} collective-permute-done((bf16[32,1792]{1,0:T(8,128)(2,1)S(1)}, bf16[32,1792]{1,0:T(8,128)(2,1)S(1)}, u32[]{:S(2)}, u32[]{:S(2)}) %collective-permute-start.3) | collective-permute-done | bytes 114720 | tf_op jit(solution)/shard_map/ppermute | solution.py:266
  13.4 1.5 %collective-permute-start.4 = (bf16[32,896]{1,0:T(8,128)(2,1)S(1)}, bf16[32,896]{1,0:T(8,128)(2,1)S(1)}, u32[]{:S(2)}, u32[]{:S(2)}) collective-permute-start(bf16[32,896]{1,0:T(8,128)(2,1)S(1)} %get-tuple-element.28), channel_id=1, source_target_pairs={{0,9},{1,8},{8,1},{9,0},{16,25},{17,24},{24,17},{25,16},{2,11},{3,... | collective-permute-start | bytes 172040 | tf_op jit(solution)/shard_map/ppermute | solution.py:273
  14.9 1.3 %collective-permute-start.5 = (bf16[32,896]{1,0:T(8,128)(2,1)S(1)}, bf16[32,896]{1,0:T(8,128)(2,1)S(1)}, u32[]{:S(2)}, u32[]{:S(2)}) collective-permute-start(bf16[32,896]{1,0:T(8,128)(2,1)S(1)} %get-tuple-element.29), channel_id=1, source_target_pairs={{0,17},{1,16},{8,25},{9,24},{16,1},{17,0},{24,9},{25,8},{2,19},{3,... | collective-permute-start | bytes 172040 | tf_op jit(solution)/shard_map/ppermute | solution.py:273
  16.2 0.4 %collective-permute-start.6 = (bf16[32,896]{1,0:T(8,128)(2,1)S(1)}, bf16[32,896]{1,0:T(8,128)(2,1)S(1)}, u32[]{:S(2)}, u32[]{:S(2)}) collective-permute-start(bf16[32,896]{1,0:T(8,128)(2,1)S(1)} %get-tuple-element.30), channel_id=1, source_target_pairs={{0,25},{1,24},{8,17},{9,16},{16,9},{17,8},{24,1},{25,0},{2,27},{3,... | collective-permute-start | bytes 172040 | tf_op jit(solution)/shard_map/ppermute | solution.py:273
  16.7 2.0 %shard_map.86.refs_6_ = bf16[3584,512]{1,0:T(8,128)(2,1)S(1)} custom-call(bf16[3584,512]{1,0:T(8,128)(2,1)} %bitcast.9, bf16[32,896]{1,0:T(8,128)(2,1)S(1)} %get-tuple-element.27.after.refs_0_), custom_call_target="tpu_custom_call" | custom-call | tf_op jit(solution)/shard_map/pallas_call | solution.py:325
  18.7 0.1 collective-permute-done.5.refs_2_
  18.8 2.0 %collective-permute-done.6.refs_3_ = bf16[32,896]{1,0:T(8,128)(2,1)S(1)} collective-permute-done((bf16[32,896]{1,0:T(8,128)(2,1)S(1)}, bf16[32,896]{1,0:T(8,128)(2,1)S(1)}, u32[]{:S(2)}, u32[]{:S(2)}) %collective-permute-start.6) | collective-permute-done | bytes 57376 | tf_op jit(solution)/shard_map/ppermute | solution.py:273
  20.8 0.6 %shard_map.87 = (f32[32,512]{1,0:T(8,128)S(1)}, bf16[32,512]{1,0:T(8,128)(2,1)S(1)}, bf16[32,512]{1,0:T(8,128)(2,1)S(1)}, bf16[32,512]{1,0:T(8,128)(2,1)S(1)}) custom-call(bf16[32,896]{1,0:T(8,128)(2,1)S(1)} %get-tuple-element.27.after.refs_0_, bf16[32,896]{1,0:T(8,128)(2,1)S(1)} %collective-permute-done.4.refs_1_, ...), custom_call_target="tpu_custom_call" | custom-call | tf_op jit(solution)/shard_map/pallas_call | solution.py:327
  21.4 0.5 %collective-permute-start.8 = (bf16[32,512]{1,0:T(8,128)(2,1)S(1)}, bf16[32,512]{1,0:T(8,128)(2,1)S(1)}, u32[]{:S(2)}, u32[]{:S(2)}) collective-permute-start(bf16[32,512]{1,0:T(8,128)(2,1)S(1)} %get-tuple-element.33), channel_id=1, source_target_pairs={{0,9},{1,8},{8,1},{9,0},{16,25},{17,24},{24,17},{25,16},{2,11},{3,... | collective-permute-start | bytes 98312 | tf_op jit(solution)/shard_map/ppermute | solution.py:273
  22.0 0.3 collective-permute-start.9
  22.3 2.3 %collective-permute-start.10 = (bf16[32,512]{1,0:T(8,128)(2,1)S(1)}, bf16[32,512]{1,0:T(8,128)(2,1)S(1)}, u32[]{:S(2)}, u32[]{:S(2)}) collective-permute-start(bf16[32,512]{1,0:T(8,128)(2,1)S(1)} %get-tuple-element.35.after), channel_id=1, source_target_pairs={{0,25},{1,24},{8,17},{9,16},{16,9},{17,8},{24,1},{25,0},{2,27},{3,... | collective-permute-start | bytes 98312 | tf_op jit(solution)/shard_map/ppermute | solution.py:273
  24.6 2.0 %shard_map.88.refs_7_ = bf16[3584,512]{1,0:T(8,128)(2,1)S(1)} custom-call(bf16[3584,512]{1,0:T(8,128)(2,1)} %bitcast.8, bf16[32,512]{1,0:T(8,128)(2,1)S(1)} %get-tuple-element.35.after), custom_call_target="tpu_custom_call" | custom-call | tf_op jit(solution)/shard_map/pallas_call | solution.py:334
  26.7 1.2 %shard_map.89 = bf16[32,1792]{1,0:T(8,128)(2,1)S(1)} custom-call(f32[32,512]{1,0:T(8,128)S(1)} %get-tuple-element.32.refs_0_, bf16[32,512]{1,0:T(8,128)(2,1)S(1)} %collective-permute-done.8.refs_1_, bf16[32,512]{1,0:T(8,128)(2,1)S(1)} %collective-permute-done.9.refs_2_, bf16[32,512]{1,0:T(8,128)(2,1)S(1)} %collective-permute-done.10.refs_3_, ...), custom_call_target="tpu_custom_call" | custom-call | tf_op jit(solution)/shard_map/pallas_call | solution.py:337
  27.9 0.2 collective-permute-start.11
  28.1 1.2 %shard_map.90 = bf16[32,1792]{1,0:T(8,128)(2,1)S(1)} custom-call(f32[32,512]{1,0:T(8,128)S(1)} %get-tuple-element.32.refs_0_, bf16[32,512]{1,0:T(8,128)(2,1)S(1)} %collective-permute-done.8.refs_1_, bf16[32,512]{1,0:T(8,128)(2,1)S(1)} %collective-permute-done.9.refs_2_, bf16[32,512]{1,0:T(8,128)(2,1)S(1)} %collective-permute-done.10.refs_3_, ...), custom_call_target="tpu_custom_call" | custom-call | tf_op jit(solution)/shard_map/pallas_call | solution.py:337
  29.2 0.0 collective-permute-done.11
  29.3 0.4 %collective-permute-start.12 = (bf16[8,1792]{1,0:T(8,128)(2,1)S(1)}, bf16[8,1792]{1,0:T(8,128)(2,1)S(1)}, u32[]{:S(2)}, u32[]{:S(2)}) collective-permute-start(bf16[8,1792]{1,0:T(8,128)(2,1)S(1)} %get-tuple-element.37), channel_id=1, source_target_pairs={{0,1},{1,0},{2,3},{3,2},{4,5},{5,4},{6,7},{7,6},{8,9},{9,8},{10,11... | collective-permute-start | bytes 86024 | tf_op jit(solution)/shard_map/ppermute | solution.py:266
  29.7 1.0 %collective-permute-start.15 = (bf16[8,1792]{1,0:T(8,128)(2,1)S(1)}, bf16[8,1792]{1,0:T(8,128)(2,1)S(1)}, u32[]{:S(2)}, u32[]{:S(2)}) collective-permute-start(bf16[8,1792]{1,0:T(8,128)(2,1)S(1)} %get-tuple-element.38), channel_id=1, source_target_pairs={{0,7},{1,6},{2,5},{3,4},{4,3},{5,2},{6,1},{7,0},{8,15},{9,14},{10,... | collective-permute-start | bytes 86024 | tf_op jit(solution)/shard_map/ppermute | solution.py:273
  30.8 2.8 %collective-permute-start.13 = (bf16[8,1792]{1,0:T(8,128)(2,1)S(1)}, bf16[8,1792]{1,0:T(8,128)(2,1)S(1)}, u32[]{:S(2)}, u32[]{:S(2)}) collective-permute-start(bf16[8,1792]{1,0:T(8,128)(2,1)S(1)} %get-tuple-element.40), channel_id=1, source_target_pairs={{0,3},{1,2},{2,1},{3,0},{4,7},{5,6},{6,5},{7,4},{8,11},{9,10},{10,... | collective-permute-start | bytes 86024 | tf_op jit(solution)/shard_map/ppermute | solution.py:273
  33.6 1.2 %collective-permute-done.15 = bf16[8,1792]{1,0:T(8,128)(2,1)S(1)} collective-permute-done((bf16[8,1792]{1,0:T(8,128)(2,1)S(1)}, bf16[8,1792]{1,0:T(8,128)(2,1)S(1)}, u32[]{:S(2)}, u32[]{:S(2)}) %collective-permute-start.15) | collective-permute-done | bytes 28704 | tf_op jit(solution)/shard_map/ppermute | solution.py:273
  34.8 1.5 %collective-permute-done.14 = bf16[8,1792]{1,0:T(8,128)(2,1)S(1)} collective-permute-done((bf16[8,1792]{1,0:T(8,128)(2,1)S(1)}, bf16[8,1792]{1,0:T(8,128)(2,1)S(1)}, u32[]{:S(2)}, u32[]{:S(2)}) %collective-permute-start.14) | collective-permute-done | bytes 28704 | tf_op jit(solution)/shard_map/ppermute | solution.py:273
  36.3 1.1 %convolution_convert_fusion = bf16[128,1792]{1,0:T(8,128)(2,1)} fusion(bf16[32,128]{1,0:T(8,128)(2,1)S(1)} %get-tuple-element.21, bf16[8,1792]{1,0:T(8,128)(2,1)S(1)} %collective-permute-done.15, bf16[8,1792]{1,0:T(8,128)(2,1)S(1)} %collective-permute-done.14, bf16[8,1792]{1,0:T(8,128)(2,1)S(1)} %collective-permute-done.13, ...), kind=kOutput, calls=%fused_computation | convolution fusion | flops 15368192 | bytes 581632 | tf_op jit(solution)/shard_map/dot_general | solution.py:348
  (12 shorter events, 0.1 us)
Async XLA Ops:
  0.0 20.8 %collective-permute-start.7 = (bf16[512,896]{1,0:T(8,128)(2,1)}, bf16[512,896]{1,0:T(8,128)(2,1)S(1)}, u32[]{:S(2)}, u32[]{:S(2)}) collective-permute-start(bf16[512,896]{1,0:T(8,128)(2,1)} %bitcast.10), channel_id=1, source_target_pairs={{0,1},{1,0},{2,3},{3,2},{4,5},{5,4},{6,7},{7,6},{8,9},{9,8},{10,11... | collective-permute-start | bytes 2752520 | tf_op jit(solution)/shard_map/ppermute | solution.py:266
  1.8 6.2 %collective-permute-start = (bf16[8,1792]{1,0:T(8,128)(2,1)S(1)}, bf16[8,1792]{1,0:T(8,128)(2,1)S(1)}, u32[]{:S(2)}, u32[]{:S(2)}) collective-permute-start(bf16[8,1792]{1,0:T(8,128)(2,1)S(1)} %get-tuple-element.24), channel_id=1, source_target_pairs={{0,3},{1,2},{2,1},{3,0},{4,7},{5,6},{6,5},{7,4},{8,11},{9,10},{10,... | collective-permute-start | bytes 86024 | tf_op jit(solution)/shard_map/ppermute | solution.py:273
  4.5 4.7 %collective-permute-start.1 = (bf16[8,1792]{1,0:T(8,128)(2,1)S(1)}, bf16[8,1792]{1,0:T(8,128)(2,1)S(1)}, u32[]{:S(2)}, u32[]{:S(2)}) collective-permute-start(bf16[8,1792]{1,0:T(8,128)(2,1)S(1)} %get-tuple-element.25), channel_id=1, source_target_pairs={{0,5},{1,4},{2,7},{3,6},{4,1},{5,0},{6,3},{7,2},{8,13},{9,12},{10,... | collective-permute-start | bytes 86024 | tf_op jit(solution)/shard_map/ppermute | solution.py:273
  6.7 5.1 %collective-permute-start.2 = (bf16[8,1792]{1,0:T(8,128)(2,1)S(1)}, bf16[8,1792]{1,0:T(8,128)(2,1)S(1)}, u32[]{:S(2)}, u32[]{:S(2)}) collective-permute-start(bf16[8,1792]{1,0:T(8,128)(2,1)S(1)} %get-tuple-element.26), channel_id=1, source_target_pairs={{0,7},{1,6},{2,5},{3,4},{4,3},{5,2},{6,1},{7,0},{8,15},{9,14},{10,... | collective-permute-start | bytes 86024 | tf_op jit(solution)/shard_map/ppermute | solution.py:273
  11.8 1.5 %collective-permute-start.3 = (bf16[32,1792]{1,0:T(8,128)(2,1)S(1)}, bf16[32,1792]{1,0:T(8,128)(2,1)S(1)}, u32[]{:S(2)}, u32[]{:S(2)}) collective-permute-start(bf16[32,1792]{1,0:T(8,128)(2,1)S(1)} %shard_map.84.own), channel_id=1, source_target_pairs={{0,1},{1,0},{2,3},{3,2},{4,5},{5,4},{6,7},{7,6},{8,9},{9,8},{10,11... | collective-permute-start | bytes 344072 | tf_op jit(solution)/shard_map/ppermute | solution.py:266
  13.4 5.3 %collective-permute-start.4 = (bf16[32,896]{1,0:T(8,128)(2,1)S(1)}, bf16[32,896]{1,0:T(8,128)(2,1)S(1)}, u32[]{:S(2)}, u32[]{:S(2)}) collective-permute-start(bf16[32,896]{1,0:T(8,128)(2,1)S(1)} %get-tuple-element.28), channel_id=1, source_target_pairs={{0,9},{1,8},{8,1},{9,0},{16,25},{17,24},{24,17},{25,16},{2,11},{3,... | collective-permute-start | bytes 172040 | tf_op jit(solution)/shard_map/ppermute | solution.py:273
  14.9 3.9 %collective-permute-start.5 = (bf16[32,896]{1,0:T(8,128)(2,1)S(1)}, bf16[32,896]{1,0:T(8,128)(2,1)S(1)}, u32[]{:S(2)}, u32[]{:S(2)}) collective-permute-start(bf16[32,896]{1,0:T(8,128)(2,1)S(1)} %get-tuple-element.29), channel_id=1, source_target_pairs={{0,17},{1,16},{8,25},{9,24},{16,1},{17,0},{24,9},{25,8},{2,19},{3,... | collective-permute-start | bytes 172040 | tf_op jit(solution)/shard_map/ppermute | solution.py:273
  16.2 4.6 %collective-permute-start.6 = (bf16[32,896]{1,0:T(8,128)(2,1)S(1)}, bf16[32,896]{1,0:T(8,128)(2,1)S(1)}, u32[]{:S(2)}, u32[]{:S(2)}) collective-permute-start(bf16[32,896]{1,0:T(8,128)(2,1)S(1)} %get-tuple-element.30), channel_id=1, source_target_pairs={{0,25},{1,24},{8,17},{9,16},{16,9},{17,8},{24,1},{25,0},{2,27},{3,... | collective-permute-start | bytes 172040 | tf_op jit(solution)/shard_map/ppermute | solution.py:273
  21.4 5.3 %collective-permute-start.8 = (bf16[32,512]{1,0:T(8,128)(2,1)S(1)}, bf16[32,512]{1,0:T(8,128)(2,1)S(1)}, u32[]{:S(2)}, u32[]{:S(2)}) collective-permute-start(bf16[32,512]{1,0:T(8,128)(2,1)S(1)} %get-tuple-element.33), channel_id=1, source_target_pairs={{0,9},{1,8},{8,1},{9,0},{16,25},{17,24},{24,17},{25,16},{2,11},{3,... | collective-permute-start | bytes 98312 | tf_op jit(solution)/shard_map/ppermute | solution.py:273
  22.0 4.7 %collective-permute-start.9 = (bf16[32,512]{1,0:T(8,128)(2,1)S(1)}, bf16[32,512]{1,0:T(8,128)(2,1)S(1)}, u32[]{:S(2)}, u32[]{:S(2)}) collective-permute-start(bf16[32,512]{1,0:T(8,128)(2,1)S(1)} %get-tuple-element.34), channel_id=1, source_target_pairs={{0,17},{1,16},{8,25},{9,24},{16,1},{17,0},{24,9},{25,8},{2,19},{3,... | collective-permute-start | bytes 98312 | tf_op jit(solution)/shard_map/ppermute | solution.py:273
  22.3 4.4 %collective-permute-start.10 = (bf16[32,512]{1,0:T(8,128)(2,1)S(1)}, bf16[32,512]{1,0:T(8,128)(2,1)S(1)}, u32[]{:S(2)}, u32[]{:S(2)}) collective-permute-start(bf16[32,512]{1,0:T(8,128)(2,1)S(1)} %get-tuple-element.35.after), channel_id=1, source_target_pairs={{0,25},{1,24},{8,17},{9,16},{16,9},{17,8},{24,1},{25,0},{2,27},{3,... | collective-permute-start | bytes 98312 | tf_op jit(solution)/shard_map/ppermute | solution.py:273
  27.9 1.4 %collective-permute-start.11 = (bf16[32,1792]{1,0:T(8,128)(2,1)S(1)}, bf16[32,1792]{1,0:T(8,128)(2,1)S(1)}, u32[]{:S(2)}, u32[]{:S(2)}) collective-permute-start(bf16[32,1792]{1,0:T(8,128)(2,1)S(1)} %shard_map.89), channel_id=1, source_target_pairs={{0,1},{1,0},{2,3},{3,2},{4,5},{5,4},{6,7},{7,6},{8,9},{9,8},{10,11... | collective-permute-start | bytes 344072 | tf_op jit(solution)/shard_map/ppermute | solution.py:266
  29.3 4.3 %collective-permute-start.12 = (bf16[8,1792]{1,0:T(8,128)(2,1)S(1)}, bf16[8,1792]{1,0:T(8,128)(2,1)S(1)}, u32[]{:S(2)}, u32[]{:S(2)}) collective-permute-start(bf16[8,1792]{1,0:T(8,128)(2,1)S(1)} %get-tuple-element.37), channel_id=1, source_target_pairs={{0,1},{1,0},{2,3},{3,2},{4,5},{5,4},{6,7},{7,6},{8,9},{9,8},{10,11... | collective-permute-start | bytes 86024 | tf_op jit(solution)/shard_map/ppermute | solution.py:266
  29.7 5.1 %collective-permute-start.15 = (bf16[8,1792]{1,0:T(8,128)(2,1)S(1)}, bf16[8,1792]{1,0:T(8,128)(2,1)S(1)}, u32[]{:S(2)}, u32[]{:S(2)}) collective-permute-start(bf16[8,1792]{1,0:T(8,128)(2,1)S(1)} %get-tuple-element.38), channel_id=1, source_target_pairs={{0,7},{1,6},{2,5},{3,4},{4,3},{5,2},{6,1},{7,0},{8,15},{9,14},{10,... | collective-permute-start | bytes 86024 | tf_op jit(solution)/shard_map/ppermute | solution.py:273
  30.8 5.6 %collective-permute-start.14 = (bf16[8,1792]{1,0:T(8,128)(2,1)S(1)}, bf16[8,1792]{1,0:T(8,128)(2,1)S(1)}, u32[]{:S(2)}, u32[]{:S(2)}) collective-permute-start(bf16[8,1792]{1,0:T(8,128)(2,1)S(1)} %get-tuple-element.39), channel_id=1, source_target_pairs={{0,5},{1,4},{2,7},{3,6},{4,1},{5,0},{6,3},{7,2},{8,13},{9,12},{10,... | collective-permute-start | bytes 86024 | tf_op jit(solution)/shard_map/ppermute | solution.py:273
  30.8 5.6 %collective-permute-start.13 = (bf16[8,1792]{1,0:T(8,128)(2,1)S(1)}, bf16[8,1792]{1,0:T(8,128)(2,1)S(1)}, u32[]{:S(2)}, u32[]{:S(2)}) collective-permute-start(bf16[8,1792]{1,0:T(8,128)(2,1)S(1)} %get-tuple-element.40), channel_id=1, source_target_pairs={{0,3},{1,2},{2,1},{3,0},{4,7},{5,6},{6,5},{7,4},{8,11},{9,10},{10,... | collective-permute-start | bytes 86024 | tf_op jit(solution)/shard_map/ppermute | solution.py:273
